TPU v7x, 256 devices: a whole 4x4x8 slice. The times are simulated.
256 devices in a mesh: section: 16 (over y, z_hi, core), rep: 4 (over z_lo), sub: 4 (over x).
Axes of the slice: x: 4, y: 4, z: 8 (z_hi: 2, z_lo: 4; z = z_hi * 4 + z_lo), core: 2. Of those that a mesh axis runs over, the one named last changes fastest.
Arguments:
- token_ids: int32 [8, 512], P(None, ('rep', 'sub')), may hold values from 0 to 255
- target_ids: int32 [8, 512], P(None, ('rep', 'sub')), may hold values from 0 to 255
- embedding: bfloat16 [256, 2048], P(('rep', 'sub')), may hold values from -3 to 3
- section_weight: bfloat16 [16, 2048, 2048], P('section', ('rep', 'sub')), may hold values from -0.125 to 0.125
- section_gain: float32 [16, 2048], P('section'), may hold values from 0.1 to 1.9
- final_gain: float32 [2048], replicated, may hold values from 0.5 to 1.5
Outputs:
- weight_grad: float32 [16, 2048, 2048], P('section', ('rep', 'sub'))
- gain_grad: float32 [16, 2048], P('section')
- embed_grad: float32 [256, 2048], P(('section', 'rep', 'sub'))
- final_grad: float32 [2048], replicated
All inputs are finite; a program needn't handle non-finite values.
Results may differ from a plain program's by a relative error of at most 0.024.
Values may be sent and summed in bfloat16 or wider, within the bound.
No kernel may reach another device: no remote copies, remote signals or barrier semaphores. Data moves between devices by JAX's collectives and lax.ppermute only.
A program may use at most 64 MiB of HBM per device.

v0:
```python
import jax
import jax.numpy as jnp
from jax import lax
from jax.sharding import PartitionSpec as P

epsilon = 1e-06
gelu_coef = 0.7978845608028654
cube_coef = 0.044715


def passed_along(value, axis, steps):
    count = lax.axis_size(axis)
    initial, last = (max(0, -steps), min(count, count - steps))
    return lax.ppermute(value, axis, [(source, source + steps) for source in range(initial, last)])


def gelu(pre_act):
    return (
        0.5
        * pre_act
        * (1.0 + jnp.tanh(gelu_coef * (pre_act + cube_coef * pre_act * pre_act * pre_act)))
    )


def gelu_slope(pre_act):
    inside = gelu_coef * (pre_act + cube_coef * pre_act * pre_act * pre_act)
    tangent = jnp.tanh(inside)
    return 0.5 * (1.0 + tangent) + 0.5 * pre_act * (1.0 - tangent * tangent) * gelu_coef * (
        1.0 + 3.0 * cube_coef * pre_act * pre_act
    )


def normalize(residual, gain_row):
    values = residual.astype(jnp.float32)
    scale_inv = lax.rsqrt(jnp.mean(values * values, axis=-1, keepdims=True) + epsilon)
    normed = values * scale_inv
    return (normed, scale_inv, (normed * gain_row).astype(jnp.bfloat16))


def norm_back(grad_norm, normed, scale_inv, gain_row):
    grad_unit = grad_norm * gain_row
    grad_in = scale_inv * (
        grad_unit - normed * jnp.mean(grad_unit * normed, axis=-1, keepdims=True)
    )
    return (grad_in, jnp.sum(grad_norm * normed, axis=0))


def pick_slot(buffer, slot_index):
    return lax.dynamic_index_in_dim(buffer, slot_index, 0, keepdims=False)


def place_slot(buffer, update, slot_index):
    return lax.dynamic_update_index_in_dim(buffer, update, slot_index, 0)


def body(token_ids, target_ids, embedding, section_weight, section_gain, final_gain):
    sections = lax.axis_size("section")
    position = lax.axis_index("section")
    micro_count = token_ids.shape[0]
    row_count = token_ids.shape[1]
    features = embedding.shape[1]
    group_size = lax.axis_size(("rep", "sub"))
    vocab_rows = embedding.shape[0] * group_size
    tick_count = micro_count + sections - 1
    contract_last = (((1,), (1,)), ((), ()))
    contract_first = (((0,), (0,)), ((), ()))
    vocab_table = lax.all_gather(embedding, ("rep", "sub"), axis=0, tiled=True)
    weight = lax.all_gather(section_weight, ("rep", "sub"), axis=1, tiled=True)[0]
    gain_row = section_gain[0]
    is_first = position == 0
    is_last = position == sections - 1
    vocab_iota = jnp.arange(vocab_rows, dtype=jnp.int32)
    onehot_in = (token_ids.reshape(-1)[:, None] == vocab_iota[None, :]).astype(jnp.bfloat16)
    embedded = jnp.dot(onehot_in, vocab_table, preferred_element_type=jnp.float32).astype(
        jnp.bfloat16
    )
    embedded = embedded.reshape(micro_count, row_count, features)
    empty_rows = jnp.zeros((row_count, features), jnp.bfloat16)
    zeros_stash = jnp.zeros((micro_count, row_count, features), jnp.bfloat16)
    zeros_pre = jnp.zeros((micro_count, row_count, features), jnp.float32)

    def forward_tick(carried, tick_index):
        arrived = carried[0]
        buffers = carried[1:]
        offset = tick_index - position
        active = (offset >= 0) & (offset < micro_count)
        slot_index = jnp.clip(offset, 0, micro_count - 1)
        residual = jnp.where(is_first, pick_slot(embedded, slot_index), arrived)

        def forward_compute(kept_activations):
            input_list, rounded_list, preactivation_list, output_list = kept_activations
            normed, scale_inv, rounded = normalize(residual, gain_row)
            pre_act = jnp.dot(rounded, weight, preferred_element_type=jnp.float32)
            returned_value = (residual.astype(jnp.float32) + gelu(pre_act)).astype(jnp.bfloat16)
            kept_activations = (
                place_slot(input_list, residual, slot_index),
                place_slot(rounded_list, rounded, slot_index),
                place_slot(preactivation_list, pre_act, slot_index),
                place_slot(output_list, returned_value, slot_index),
            )
            return (kept_activations, returned_value)

        def forward_bypass(kept_activations):
            return (kept_activations, empty_rows)

        buffers, returned_value = lax.cond(active, forward_compute, forward_bypass, buffers)
        arrived = passed_along(returned_value, "section", 1)
        return ((arrived,) + buffers, None)

    start_state = (empty_rows, zeros_stash, zeros_stash, zeros_pre, zeros_stash)
    final_state, unused_out = lax.scan(
        forward_tick, start_state, jnp.arange(tick_count, dtype=jnp.int32)
    )
    input_list, rounded_list, preactivation_list, output_list = final_state[1:]
    logit_scale = float(features) ** (-0.5)

    def head(finals):
        normed, scale_inv, final_rows = normalize(finals, final_gain)
        logits = (
            lax.dot_general(
                final_rows, vocab_table, contract_last, preferred_element_type=jnp.float32
            )
            * logit_scale
        )
        exp_logit = jnp.exp(logits)
        probability = exp_logit / jnp.sum(exp_logit, axis=-1, keepdims=True)
        onehot_out = (target_ids.reshape(-1)[:, None] == vocab_iota[None, :]).astype(jnp.float32)
        grad_logit = ((probability - onehot_out) * logit_scale).astype(jnp.bfloat16)
        embed_head = lax.dot_general(
            grad_logit, final_rows, contract_first, preferred_element_type=jnp.float32
        )
        grad_final = jnp.dot(grad_logit, vocab_table, preferred_element_type=jnp.float32)
        grad_in, final_part = norm_back(grad_final, normed, scale_inv, final_gain)
        grad_top = grad_in.astype(jnp.bfloat16).reshape(micro_count, row_count, features)
        return (embed_head, grad_top, final_part)

    def no_head(finals):
        return (
            jnp.zeros((vocab_rows, features), jnp.float32),
            zeros_stash,
            jnp.zeros((features,), jnp.float32),
        )

    embed_head, grad_top, final_part = lax.cond(
        is_last, head, no_head, output_list.reshape(-1, features)
    )

    def backward_tick(carried, tick_index):
        arrived = carried[0]
        buffers = carried[1:]
        offset = tick_index - (sections - 1 - position)
        active = (offset >= 0) & (offset < micro_count)
        slot_index = jnp.clip(offset, 0, micro_count - 1)
        grad_out = jnp.where(is_last, pick_slot(grad_top, slot_index), arrived)

        def backward_compute(kept_activations):
            preactivation_gradients, first_row_gradients, gain_accumulated = kept_activations
            grad_float = grad_out.astype(jnp.float32)
            grad_pre = (grad_float * gelu_slope(pick_slot(preactivation_list, slot_index))).astype(
                jnp.bfloat16
            )
            grad_norm = lax.dot_general(
                grad_pre, weight, contract_last, preferred_element_type=jnp.float32
            )
            normed, scale_inv, rounded = normalize(pick_slot(input_list, slot_index), gain_row)
            grad_in, gain_part = norm_back(grad_norm, normed, scale_inv, gain_row)
            sent_output = (grad_float + grad_in).astype(jnp.bfloat16)
            kept_activations = (
                place_slot(preactivation_gradients, grad_pre, slot_index),
                place_slot(first_row_gradients, sent_output, slot_index),
                gain_accumulated + gain_part,
            )
            return (kept_activations, sent_output)

        def backward_bypass(kept_activations):
            return (kept_activations, empty_rows)

        buffers, sent_output = lax.cond(active, backward_compute, backward_bypass, buffers)
        arrived = passed_along(sent_output, "section", -1)
        return ((arrived,) + buffers, None)

    back_state = (empty_rows, zeros_stash, zeros_stash, jnp.zeros((features,), jnp.float32))
    back_final, unused_back = lax.scan(
        backward_tick, back_state, jnp.arange(tick_count, dtype=jnp.int32)
    )
    preactivation_gradients, first_row_gradients, gain_accumulated = back_final[1:]
    pres_flat = preactivation_gradients.reshape(-1, features)
    rounded_flat = rounded_list.reshape(-1, features)
    weight_part = lax.psum_scatter(
        lax.dot_general(
            rounded_flat, pres_flat, contract_first, preferred_element_type=jnp.float32
        ).astype(jnp.bfloat16),
        ("rep", "sub"),
        scatter_dimension=0,
        tiled=True,
    ).astype(jnp.float32)
    gain_total = lax.psum(gain_accumulated, ("rep", "sub"))
    final_total = lax.psum(final_part, ("section", "rep", "sub"))
    embed_in = lax.dot_general(
        onehot_in,
        first_row_gradients.reshape(-1, features),
        contract_first,
        preferred_element_type=jnp.float32,
    )
    contribution = jnp.where(is_first, embed_in, 0.0) + embed_head
    embed_total = lax.psum_scatter(
        contribution, ("section", "rep", "sub"), scatter_dimension=0, tiled=True
    )
    return (weight_part[None], gain_total[None], embed_total, final_total)


def solution(mesh):
    in_specs = (
        P(None, ("rep", "sub")),
        P(None, ("rep", "sub")),
        P(("rep", "sub"), None),
        P("section", ("rep", "sub"), None),
        P("section", None),
        P(),
    )
    out_specs = (
        P("section", ("rep", "sub"), None),
        P("section", None),
        P(("section", "rep", "sub"), None),
        P(),
    )
    return jax.shard_map(body, mesh=mesh, in_specs=in_specs, out_specs=out_specs, check_vma=False)
```

profile of v0, /device:TPU:8, one launch (start us, length us, event | category | flops | bytes accessed | tf_op | source)
XLA Modules:
  0.0 1360.2 jit_solution(7029663618918827461)
XLA Ops:
  9.5 84.1 %all-gather.3.cloned.1.call-done = bf16[256,2048]{1,0:T(8,128)(2,1)} async-done(((bf16[16,2048]{1,0:T(8,128)(2,1)}), bf16[256,2048]{1,0:T(8,128)(2,1)}) %all-gather.3.cloned.1.call-update) | async-done | bytes 1048592 | tf_op jit(solution)/shard_map/all_gather | solution.py:67
  96.3 99.8 %all-gather.5.cloned.1.call-done = bf16[1,2048,2048]{2,1,0:T(8,128)(2,1)} async-done(((bf16[1,128,2048]{2,1,0:T(8,128)(2,1)}), bf16[1,2048,2048]{2,1,0:T(8,128)(2,1)}) %all-gather.5.cloned.1.call-update) | async-done | bytes 8388624 | tf_op jit(solution)/shard_map/all_gather | solution.py:68
  199.0 350.3 %while.36 = (s32[]{:T(128)}, bf16[32,2048]{1,0:T(8,128)(2,1)S(1)}, bf16[8,32,2048]{2,1,0:T(8,128)(2,1)S(1)}, bf16[8,32,2048]{2,1,0:T(8,128)(2,1)}, f32[8,32,2048...) while((s32[]{:T(128)}, bf16[32,2048]{1,0:T(8,128)(2,1)S(1)}, ...), condition=%wide.region_4.5_spmd, body=%wide.region_0.4_spmd.sunk | while | flops 269877280 | bytes 10897188 | solution.py:111
  202.2 10.6 collective-permute-done
  216.0 10.6 collective-permute-done
  229.8 9.2 collective-permute-done
  242.2 11.5 collective-permute-done
  264.3 9.2 collective-permute-done
  303.8 9.2 collective-permute-done
  402.5 9.8 collective-permute-done
  415.6 9.5 collective-permute-done
  428.4 9.3 collective-permute-done
  440.9 9.2 collective-permute-done
  453.3 9.2 collective-permute-done
  553.5 419.2 %while.37 = (s32[]{:T(128)}, bf16[32,2048]{1,0:T(8,128)(2,1)S(1)}, bf16[8,32,2048]{2,1,0:T(8,128)(2,1)}, bf16[8,32,2048]{2,1,0:T(8,128)(2,1)}, f32[2048]{0:T(102...) while((s32[]{:T(128)}, bf16[32,2048]{1,0:T(8,128)(2,1)S(1)}, ...), condition=%wide.region_17.18_spmd, body=%wide.region_11.17_spmd.sunk | while | flops 271122464 | bytes 11323943 | solution.py:183
  680.6 60.2 %collective-permute-done.1 = bf16[32,2048]{1,0:T(8,128)(2,1)S(1)} collective-permute-done((bf16[32,2048]{1,0:T(8,128)(2,1)S(1)}, bf16[32,2048]{1,0:T(8,128)(2,1)S(1)}, u32[]{:S(2)}, u32[]{:S(2)}) %collective-permute-start.1) | collective-permute-done | bytes 131104 | tf_op jit(solution)/shard_map/while/body/eval_jaxpr/ppermute | solution.py:14
  742.0 9.8 conditional.7
  753.7 9.2 collective-permute-done.1
  764.2 9.8 conditional.7
  775.9 9.2 collective-permute-done.1
  786.3 9.8 conditional.7
  808.5 9.8 conditional.7
  830.6 9.8 conditional.7
  852.8 9.8 conditional.7
  874.9 9.8 conditional.7
  886.6 10.3 collective-permute-done.1
  898.2 9.8 conditional.7
  913.7 18.4 %collective-permute-start.1 = (bf16[32,2048]{1,0:T(8,128)(2,1)S(1)}, bf16[32,2048]{1,0:T(8,128)(2,1)S(1)}, u32[]{:S(2)}, u32[]{:S(2)}) collective-permute-start(bf16[32,2048]{1,0:T(8,128)(2,1)S(1)} %get-tuple-element.740), channel_id=1, source_target_pairs={{16,0},{32,16},{48,32},{64,48},{80,64},{96,80},{112,96},{128,112},... | collective-permute-start | bytes 393224 | tf_op jit(solution)/shard_map/while/body/eval_jaxpr/ppermute | solution.py:14
  983.0 82.7 %psum.15 = f32[2048]{0:T(1024)} all-reduce(f32[2048]{0:T(1024)S(1)} %get-tuple-element.500), channel_id=1, replica_groups=mesh['section'=16,'rep'=4,'sub'=4] {'section','rep','sub'}, use_global_device_ids=true, to_apply=%region_21.22 | all-reduce | flops 2048 | bytes 16384 | tf_op jit(solution)/shard_map/psum | solution.py:198
  1065.7 40.4 %psum.14 = f32[1,2048]{1,0:T(1,128)} all-reduce(f32[1,2048]{1,0:T(1,128)S(1)} %bitcast.89), channel_id=1, replica_groups=mesh['section'=16,'rep'=4,'sub'=4] {'rep','sub'}, use_global_device_ids=true, to_apply=%region_19.20 | all-reduce | flops 2048 | bytes 16384 | tf_op jit(solution)/shard_map/psum | solution.py:197
  1106.1 136.6 %all-reduce.3.cloned.1.call-done = f32[256,2048]{1,0:T(8,128)} async-done(((f32[256,2048]{1,0:T(8,128)}), f32[256,2048]{1,0:T(8,128)}) %all-reduce.3.cloned.1.call-update) | async-done | bytes 2097168
  1244.2 107.4 %reduce-scatter.2.cloned.1.call-done = bf16[128,2048]{1,0:T(8,128)(2,1)} async-done(((bf16[2048,2048]{1,0:T(8,128)(2,1)}), bf16[128,2048]{1,0:T(8,128)(2,1)}) %reduce-scatter.2.cloned.1.call-update) | async-done | bytes 524304 | tf_op jit(solution)/shard_map/reduce_scatter | solution.py:189
  (326 shorter events, 610.5 us)
Async XLA Ops:
  7.2 86.4 %all-gather.3.cloned.1.call-start = ((), (), s32[]{:S(2)}) async-start(), calls=%async_computation.1 | async-start | bytes 1114112 | tf_op jit(solution)/shard_map/all_gather | solution.py:67
  7.9 188.1 %all-gather.5.cloned.1.call-start = ((), (), s32[]{:S(2)}) async-start(), calls=%async_computation.2 | async-start | bytes 8912896 | tf_op jit(solution)/shard_map/all_gather | solution.py:68
  8.6 1234.1 %all-reduce.3.cloned.1.call-start = ((), (), s32[]{:S(2)}) async-start(), calls=%async_computation.4 | async-start | bytes 4194304
  200.3 12.5 collective-permute-start
  214.1 12.5 collective-permute-start
  227.9 11.1 collective-permute-start
  240.3 13.4 collective-permute-start
  400.6 11.7 collective-permute-start
  413.7 11.5 collective-permute-start
  426.4 11.2 collective-permute-start
  438.9 11.1 collective-permute-start
  451.4 11.1 collective-permute-start
  476.2 11.1 collective-permute-start
  488.6 11.1 collective-permute-start
  501.0 11.1 collective-permute-start
  560.5 11.1 collective-permute-start.1
  572.9 11.1 collective-permute-start.1
  585.3 11.1 collective-permute-start.1
  597.7 11.1 collective-permute-start.1
  610.1 11.1 collective-permute-start.1
  622.4 11.1 collective-permute-start.1
  634.8 11.1 collective-permute-start.1
  647.2 11.1 collective-permute-start.1
  659.6 11.1 collective-permute-start.1
  672.0 68.8 %collective-permute-start.1 = (bf16[32,2048]{1,0:T(8,128)(2,1)S(1)}, bf16[32,2048]{1,0:T(8,128)(2,1)S(1)}, u32[]{:S(2)}, u32[]{:S(2)}) collective-permute-start(bf16[32,2048]{1,0:T(8,128)(2,1)S(1)} %get-tuple-element.740), channel_id=1, source_target_pairs={{16,0},{32,16},{48,32},{64,48},{80,64},{96,80},{112,96},{128,112},... | collective-permute-start | bytes 393224 | tf_op jit(solution)/shard_map/while/body/eval_jaxpr/ppermute | solution.py:14
  751.8 11.1 collective-permute-start.1
  884.7 12.3 collective-permute-start.1
  913.7 21.7 %collective-permute-start.1 = (bf16[32,2048]{1,0:T(8,128)(2,1)S(1)}, bf16[32,2048]{1,0:T(8,128)(2,1)S(1)}, u32[]{:S(2)}, u32[]{:S(2)}) collective-permute-start(bf16[32,2048]{1,0:T(8,128)(2,1)S(1)} %get-tuple-element.740), channel_id=1, source_target_pairs={{16,0},{32,16},{48,32},{64,48},{80,64},{96,80},{112,96},{128,112},... | collective-permute-start | bytes 393224 | tf_op jit(solution)/shard_map/while/body/eval_jaxpr/ppermute | solution.py:14
  936.7 11.1 collective-permute-start.1
  949.1 11.1 collective-permute-start.1
  961.5 11.1 collective-permute-start.1
  975.8 375.7 %reduce-scatter.2.cloned.1.call-start = ((), (), s32[]{:S(2)}) async-start(), calls=%async_computation.3 | async-start | bytes 8912896 | tf_op jit(solution)/shard_map/reduce_scatter | solution.py:189
  (27 other events, 1917.6 us)
Sparse Core Ops, SparseCore 0:
  9.8 83.7 all-gather.2
  95.4 100.6 all-gather.4
  975.9 266.7 all-reduce.2
  1245.1 106.3 reduce-scatter.1
where the time goes:
time: 1360 us
  waiting for transfers between devices  810 us (60%)
  starting transfers between devices  191 us (14%)
  blocking collectives  123 us (9%)
  matrix products  105 us (8%)
  local copies, waits for them, and re-layouts  44.2 us (3%)
  other arithmetic  40.1 us (3%)
  loops' own time  32.3 us (2%)
  between operations  13.9 us (1%)
    ppermute x46, waiting for transfers between devices, passed_along(): lax.ppermute(value, axis, [(source, source + steps) for source in range(i...  381 us
    ppermute x46, starting transfers between devices, passed_along(): lax.ppermute(value, axis, [(source, source + steps) for source in range(i...  191 us
    unnamed x5, waiting for transfers between devices  138 us
    reduce_scatter x1, waiting for transfers between devices, body(): lax.psum_scatter(lax.dot_general(rounded_flat, pres_flat, contract_first,...  107 us
    all_gather x1, waiting for transfers between devices, body(): lax.all_gather(section_weight, ('rep', 'sub'), axis=1, tiled=True)[0]  99.8 us
    all_gather x1, waiting for transfers between devices, body(): vocab_table = lax.all_gather(embedding, ('rep', 'sub'), axis=0, tiled=True)  84.1 us
    psum x1, blocking collectives, body(): final_total = lax.psum(final_part, ('section', 'rep', 'sub'))  82.7 us
    dot_general x8, matrix products, backward_compute(): lax.dot_general(grad_pre, weight, contract_last, preferred_element_type=j...  48.8 us
  transfers between devices with their start and end apart: 50, of which 50 were waited for; matrix products, arithmetic and copies ran while one was open for 1% of the time, Pallas kernels for 0%

commit v1 on v0

--- a/solution.py
+++ b/solution.py
@@ -64,7 +64,12 @@
     tick_count = micro_count + sections - 1
     contract_last = (((1,), (1,)), ((), ()))
     contract_first = (((0,), (0,)), ((), ()))
-    vocab_table = lax.all_gather(embedding, ("rep", "sub"), axis=0, tiled=True)
+    vocab_table = jnp.concatenate(
+        lax.all_to_all(
+            jnp.stack([embedding] * lax.axis_size(("rep", "sub"))), ("rep", "sub"), 0, 0
+        ),
+        axis=0,
+    )
     weight = lax.all_gather(section_weight, ("rep", "sub"), axis=1, tiled=True)[0]
     gain_row = section_gain[0]
     is_first = position == 0

time: 1360 us -> 1300 us (0.956)
  waiting for transfers between devices: 810 us -> 734 us
    all_to_all x0 -> x1, waiting for transfers between devices: none -> 109 us  [body(): lax.all_to_all(jnp.stack([embedding] * lax.axis_size(('rep', 'sub'))), ('...]
    all_gather x1, waiting for transfers between devices: 99.8 us -> 0.01 us  [body(): lax.all_gather(section_weight, ('rep', 'sub'), axis=1, tiled=True)[0]]
    all_gather x1 -> x0, waiting for transfers between devices: 84.1 us -> none  [body(): vocab_table = lax.all_gather(embedding, ('rep', 'sub'), axis=0, tiled=True)]
    unnamed x5 -> x4, waiting for transfers between devices: 138 us -> 136 us
  transfers between devices with their start and end apart: 50 -> 50, of which waited for: 50 -> 49; matrix products, arithmetic and copies ran while one was open for 1% -> 1% of each run, Pallas kernels for 0% -> 0%
where the time goes in v1:
time: 1300 us
  waiting for transfers between devices  734 us (56%)
  starting transfers between devices  200 us (15%)
  blocking collectives  130 us (10%)
  matrix products  103 us (8%)
  local copies, waits for them, and re-layouts  44.9 us (3%)
  other arithmetic  42.6 us (3%)
  loops' own time  30.8 us (2%)
  between operations  13.9 us (1%)
    ppermute x46, waiting for transfers between devices, passed_along(): lax.ppermute(value, axis, [(source, source + steps) for source in range(i...  382 us
    ppermute x46, starting transfers between devices, passed_along(): lax.ppermute(value, axis, [(source, source + steps) for source in range(i...  192 us
    unnamed x4, waiting for transfers between devices  136 us
    all_to_all x1, waiting for transfers between devices, body(): lax.all_to_all(jnp.stack([embedding] * lax.axis_size(('rep', 'sub'))), ('...  109 us
    reduce_scatter x1, waiting for transfers between devices, body(): lax.psum_scatter(lax.dot_general(rounded_flat, pres_flat, contract_first,...  107 us
    psum x1, blocking collectives, body(): final_total = lax.psum(final_part, ('section', 'rep', 'sub'))  86.4 us
    dot_general x8, matrix products, backward_compute(): lax.dot_general(grad_pre, weight, contract_last, preferred_element_type=j...  48.9 us
    dot_general x8, matrix products, forward_compute(): pre_act = jnp.dot(rounded, weight, preferred_element_type=jnp.float32)  44.8 us
  transfers between devices with their start and end apart: 50, of which 49 were waited for; matrix products, arithmetic and copies ran while one was open for 1% of the time, Pallas kernels for 0%

profile of v1, /device:TPU:8, one launch (start us, length us, event | category | flops | bytes accessed | tf_op | source)
XLA Modules:
  0.0 1299.0 jit_solution(17838747183885664201)
XLA Ops:
  18.5 108.7 %all-to-all-done = bf16[16,16,2048]{2,1,0:T(8,128)(2,1)S(1)} async-done(((bf16[16,16,2048]{2,1,0:T(8,128)(2,1)}), bf16[16,16,2048]{2,1,0:T(8,128)(2,1)S(1)}, u32[]{:S(2)}, u32[]{:S(2)}) %all-to-all-start) | async-done | bytes 1048608 | tf_op jit(solution)/shard_map/all_to_all | solution.py:68
  131.6 348.6 %while.36 = (s32[]{:T(128)}, bf16[32,2048]{1,0:T(8,128)(2,1)S(1)}, bf16[8,32,2048]{2,1,0:T(8,128)(2,1)S(1)}, bf16[8,32,2048]{2,1,0:T(8,128)(2,1)}, f32[8,32,2048...) while((s32[]{:T(128)}, bf16[32,2048]{1,0:T(8,128)(2,1)S(1)}, ...), condition=%wide.region_4.5_spmd, body=%wide.region_0.4_spmd.sunk | while | flops 269877280 | bytes 10897188 | solution.py:116
  134.8 9.2 collective-permute-done
  147.2 9.2 collective-permute-done
  159.5 9.2 collective-permute-done
  171.8 14.2 %collective-permute-done = bf16[32,2048]{1,0:T(8,128)(2,1)S(1)} collective-permute-done((bf16[32,2048]{1,0:T(8,128)(2,1)S(1)}, bf16[32,2048]{1,0:T(8,128)(2,1)S(1)}, u32[]{:S(2)}, u32[]{:S(2)}) %collective-permute-start) | collective-permute-done | bytes 131104 | tf_op jit(solution)/shard_map/while/body/eval_jaxpr/ppermute | solution.py:14
  216.2 9.2 collective-permute-done
  235.8 9.2 collective-permute-done
  255.5 9.2 collective-permute-done
  275.1 9.2 collective-permute-done
  294.8 9.2 collective-permute-done
  314.5 10.7 collective-permute-done
  335.6 9.3 collective-permute-done
  348.0 9.2 collective-permute-done
  360.3 9.2 collective-permute-done
  484.4 423.2 %while.37 = (s32[]{:T(128)}, bf16[32,2048]{1,0:T(8,128)(2,1)S(1)}, bf16[8,32,2048]{2,1,0:T(8,128)(2,1)}, bf16[8,32,2048]{2,1,0:T(8,128)(2,1)S(1)}, f32[2048]{0:T...) while((s32[]{:T(128)}, bf16[32,2048]{1,0:T(8,128)(2,1)S(1)}, ...), condition=%wide.region_17.18_spmd, body=%wide.region_11.17_spmd.sunk | while | flops 271122464 | bytes 11324200 | solution.py:188
  611.6 63.0 %collective-permute-done.1 = bf16[32,2048]{1,0:T(8,128)(2,1)S(1)} collective-permute-done((bf16[32,2048]{1,0:T(8,128)(2,1)S(1)}, bf16[32,2048]{1,0:T(8,128)(2,1)S(1)}, u32[]{:S(2)}, u32[]{:S(2)}) %collective-permute-start.1) | collective-permute-done | bytes 131104 | tf_op jit(solution)/shard_map/while/body/eval_jaxpr/ppermute | solution.py:14
  675.8 10.1 conditional.7
  687.9 9.2 collective-permute-done.1
  698.4 10.2 conditional.7
  720.8 10.1 conditional.7
  743.3 10.1 conditional.7
  765.8 10.2 conditional.7
  788.4 10.2 conditional.7
  800.5 9.2 collective-permute-done.1
  810.9 10.2 conditional.7
  833.3 10.1 conditional.7
  849.2 18.7 %collective-permute-start.1 = (bf16[32,2048]{1,0:T(8,128)(2,1)S(1)}, bf16[32,2048]{1,0:T(8,128)(2,1)S(1)}, u32[]{:S(2)}, u32[]{:S(2)}) collective-permute-start(bf16[32,2048]{1,0:T(8,128)(2,1)S(1)} %get-tuple-element.740), channel_id=1, source_target_pairs={{16,0},{32,16},{48,32},{64,48},{80,64},{96,80},{112,96},{128,112},... | collective-permute-start | bytes 393224 | tf_op jit(solution)/shard_map/while/body/eval_jaxpr/ppermute | solution.py:14
  916.7 86.4 %psum.15 = f32[2048]{0:T(1024)} all-reduce(f32[2048]{0:T(1024)S(1)} %get-tuple-element.500), channel_id=1, replica_groups=mesh['section'=16,'rep'=4,'sub'=4] {'section','rep','sub'}, use_global_device_ids=true, to_apply=%region_21.22 | all-reduce | flops 2048 | bytes 16384 | tf_op jit(solution)/shard_map/psum | solution.py:203
  1003.1 43.1 %psum.14 = f32[1,2048]{1,0:T(1,128)} all-reduce(f32[1,2048]{1,0:T(1,128)S(1)} %bitcast.91), channel_id=1, replica_groups=mesh['section'=16,'rep'=4,'sub'=4] {'rep','sub'}, use_global_device_ids=true, to_apply=%region_19.20 | all-reduce | flops 2048 | bytes 16384 | tf_op jit(solution)/shard_map/psum | solution.py:202
  1046.2 135.3 %all-reduce.3.cloned.1.call-done = f32[256,2048]{1,0:T(8,128)} async-done(((f32[256,2048]{1,0:T(8,128)}), f32[256,2048]{1,0:T(8,128)}) %all-reduce.3.cloned.1.call-update) | async-done | bytes 2097168
  1182.9 107.5 %reduce-scatter.2.cloned.1.call-done = bf16[128,2048]{1,0:T(8,128)(2,1)} async-done(((bf16[2048,2048]{1,0:T(8,128)(2,1)}), bf16[128,2048]{1,0:T(8,128)(2,1)}) %reduce-scatter.2.cloned.1.call-update) | async-done | bytes 524304 | tf_op jit(solution)/shard_map/reduce_scatter | solution.py:194
  (326 shorter events, 609.4 us)
Async XLA Ops:
  7.2 121.5 %all-gather.2.cloned.1.call-start = ((), (), s32[]{:S(2)}) async-start(), calls=%async_computation.2 | async-start | bytes 8912896 | tf_op jit(solution)/shard_map/all_gather | solution.py:73
  9.8 117.3 %all-to-all-start = ((bf16[16,16,2048]{2,1,0:T(8,128)(2,1)}), bf16[16,16,2048]{2,1,0:T(8,128)(2,1)S(1)}, u32[]{:S(2)}, u32[]{:S(2)}) async-start(bf16[16,16,2048]{2,1,0:T(8,128)(2,1)} %stack.2), calls=%async_computation | async-start | bytes 2097152 | tf_op jit(solution)/shard_map/all_to_all | solution.py:68
  18.3 1163.1 %all-reduce.3.cloned.1.call-start = ((), (), s32[]{:S(2)}) async-start(), calls=%async_computation.4 | async-start | bytes 4194304
  132.9 11.2 collective-permute-start
  145.2 11.1 collective-permute-start
  157.6 11.1 collective-permute-start
  169.9 16.2 %collective-permute-start = (bf16[32,2048]{1,0:T(8,128)(2,1)S(1)}, bf16[32,2048]{1,0:T(8,128)(2,1)S(1)}, u32[]{:S(2)}, u32[]{:S(2)}) collective-permute-start(bf16[32,2048]{1,0:T(8,128)(2,1)S(1)} %get-tuple-element.722), channel_id=1, source_target_pairs={{0,16},{16,32},{32,48},{48,64},{64,80},{80,96},{96,112},{112,128},... | collective-permute-start | bytes 393224 | tf_op jit(solution)/shard_map/while/body/eval_jaxpr/ppermute | solution.py:14
  312.5 12.6 collective-permute-start
  333.7 11.2 collective-permute-start
  346.1 11.1 collective-permute-start
  358.4 11.1 collective-permute-start
  383.0 11.1 collective-permute-start
  491.5 11.1 collective-permute-start.1
  503.9 11.1 collective-permute-start.1
  516.3 11.1 collective-permute-start.1
  528.6 11.1 collective-permute-start.1
  541.1 11.1 collective-permute-start.1
  553.5 11.1 collective-permute-start.1
  565.8 11.1 collective-permute-start.1
  578.2 11.1 collective-permute-start.1
  590.6 11.1 collective-permute-start.1
  603.0 71.6 %collective-permute-start.1 = (bf16[32,2048]{1,0:T(8,128)(2,1)S(1)}, bf16[32,2048]{1,0:T(8,128)(2,1)S(1)}, u32[]{:S(2)}, u32[]{:S(2)}) collective-permute-start(bf16[32,2048]{1,0:T(8,128)(2,1)S(1)} %get-tuple-element.740), channel_id=1, source_target_pairs={{16,0},{32,16},{48,32},{64,48},{80,64},{96,80},{112,96},{128,112},... | collective-permute-start | bytes 393224 | tf_op jit(solution)/shard_map/while/body/eval_jaxpr/ppermute | solution.py:14
  686.0 11.2 collective-permute-start.1
  731.0 11.1 collective-permute-start.1
  753.5 11.1 collective-permute-start.1
  776.0 11.1 collective-permute-start.1
  798.5 11.1 collective-permute-start.1
  849.2 21.2 %collective-permute-start.1 = (bf16[32,2048]{1,0:T(8,128)(2,1)S(1)}, bf16[32,2048]{1,0:T(8,128)(2,1)S(1)}, u32[]{:S(2)}, u32[]{:S(2)}) collective-permute-start(bf16[32,2048]{1,0:T(8,128)(2,1)S(1)} %get-tuple-element.740), channel_id=1, source_target_pairs={{16,0},{32,16},{48,32},{64,48},{80,64},{96,80},{112,96},{128,112},... | collective-permute-start | bytes 393224 | tf_op jit(solution)/shard_map/while/body/eval_jaxpr/ppermute | solution.py:14
  871.7 11.1 collective-permute-start.1
  884.1 11.1 collective-permute-start.1
  896.5 11.1 collective-permute-start.1
  909.5 380.9 %reduce-scatter.2.cloned.1.call-start = ((), (), s32[]{:S(2)}) async-start(), calls=%async_computation.3 | async-start | bytes 8912896 | tf_op jit(solution)/shard_map/reduce_scatter | solution.py:194
  (27 other events, 1324.7 us)
Sparse Core Ops, SparseCore 0:
  9.8 116.7 all-gather.1
  909.6 271.7 all-reduce.2
  1184.0 106.3 reduce-scatter.1
